TPU v7x, 32 devices: a whole 2x2x4 slice. The times are simulated.
32 devices in a mesh: row: 8 (over z, y), col: 4 (over x, core).
Axes of the slice: x: 2, y: 2, z: 4, core: 2. Of those that a mesh axis runs over, the one named last changes fastest.
Arguments:
- matrix: float32 [4096, 4096], P('row', 'col'), may hold values from -0.92 to 1.92, as said below
Outputs:
- inverse: float32 [4096, 4096], P('row', 'col')
- residual_norms: float32 [4], replicated
Inputs may be any that keep to these rules, and one draw needn't show every extreme that they name: matrix is exactly symmetric and positive definite; all its eigenvalues lie between 0.08 and 1.92.
All inputs are finite; a program needn't handle non-finite values.
Results may differ from a plain program's by a relative error of at most 0.0017.
The roundings to bfloat16 on the way count: a program that leaves them out, or rounds other values in their place, can miss the bound.
Values may be sent and summed in bfloat16 or wider, within the bound.
A program may use at most 64 MiB of HBM per device.

v0:
```python
import jax
import jax.numpy as jnp
from jax import lax
from jax.sharding import PartitionSpec as P

N = 4096
ITERS = 4


def shards(matrix):
    row_count, col_count = matrix.shape
    row_index = lax.axis_index("row")
    col_index = lax.axis_index("col")
    sq_total = lax.psum(jnp.sum(matrix * matrix), ("row", "col"))
    start_scale = jnp.sqrt(jnp.float32(N)) / jnp.sqrt(sq_total)
    global_rows = row_index * row_count + lax.broadcasted_iota(jnp.int32, (row_count, col_count), 0)
    global_cols = col_index * col_count + lax.broadcasted_iota(jnp.int32, (row_count, col_count), 1)
    eye_block = (global_rows == global_cols).astype(jnp.float32)
    mat_low = matrix.astype(jnp.bfloat16)
    panel_rows = lax.all_gather(mat_low, "col", axis=1, tiled=True)
    current = start_scale * eye_block
    partial_list = []
    for iteration in range(ITERS):
        cur_low = current.astype(jnp.bfloat16)
        product = jnp.dot(
            panel_rows,
            lax.all_gather(cur_low, "row", axis=0, tiled=True),
            preferred_element_type=jnp.float32,
        )
        residual = eye_block - product
        local_sum = jnp.sum(residual * residual)
        partial_list.append(local_sum)
        shift_low = (eye_block + residual).astype(jnp.bfloat16)
        iterate_rows = lax.all_gather(cur_low, "col", axis=1, tiled=True)
        current = jnp.dot(
            iterate_rows,
            lax.all_gather(shift_low, "row", axis=0, tiled=True),
            preferred_element_type=jnp.float32,
        )
    summed = lax.psum(jnp.stack(partial_list), ("row", "col"))
    residual_norms = jnp.sqrt(summed / N)
    return (current, residual_norms)


def solution(mesh):
    in_specs = (P("row", "col"),)
    out_specs = (P("row", "col"), P())
    return jax.shard_map(shards, mesh=mesh, in_specs=in_specs, out_specs=out_specs, check_vma=False)
```

profile of v0, /device:TPU:0, one launch (start us, length us, event | category | flops | bytes accessed | tf_op | source)
XLA Modules:
  0.0 1244.4 jit_solution(14768718448786911574)
XLA Ops:
  7.2 0.0 all-gather.18.cloned.1.call-start
  7.2 4.3 fusion.5
  11.5 0.0 all-gather.18.cloned.1.call-update
  11.5 0.0 all-gather.16.cloned.1.call-start
  11.6 42.5 %psum.14 = f32[]{:T(128)} all-reduce(f32[]{:T(128)} %get-tuple-element.8), channel_id=1, replica_groups=mesh['row'=8,'col'=4] {'row','col'}, use_global_device_ids=true, to_apply=%region_1.0 | all-reduce | flops 1 | bytes 8 | tf_op jit(solution)/shard_map/psum | solution.py:14
  54.8 1.2 fusion
  56.0 0.0 all-gather.16.cloned.1.call-update
  56.1 0.0 all-gather.14.cloned.1.call-start
  56.1 0.7 all-gather.14.cloned.1.call-update
  56.8 0.0 all-gather.20.cloned.1.call-start
  56.9 0.0 all-gather.18.cloned.1.call-done
  56.9 124.6 %all-gather.16.cloned.1.call-done = bf16[4096,1024]{0,1:T(8,128)(2,1)} async-done(((bf16[512,1024]{0,1:T(8,128)(2,1)}), bf16[4096,1024]{0,1:T(8,128)(2,1)}) %all-gather.16.cloned.1.call-update) | async-done | bytes 8388624 | tf_op jit(solution)/shard_map/all_gather | solution.py:27
  181.5 10.1 fusion.1
  191.6 0.0 all-gather.24.cloned.1.call-start
  191.7 24.1 %all-gather.14.cloned.1.call-done = bf16[512,4096]{0,1:T(8,128)(2,1)} async-done(((bf16[512,1024]{0,1:T(8,128)(2,1)}), bf16[512,4096]{0,1:T(8,128)(2,1)}) %all-gather.14.cloned.1.call-update) | async-done | bytes 4194320 | tf_op jit(solution)/shard_map/all_gather | solution.py:34
  215.7 127.4 %all-gather.20.cloned.1.call-done = bf16[4096,1024]{0,1:T(8,128)(2,1)} async-done(((bf16[512,1024]{0,1:T(8,128)(2,1)}), bf16[4096,1024]{0,1:T(8,128)(2,1)}) %all-gather.20.cloned.1.call-update) | async-done | bytes 8388624 | tf_op jit(solution)/shard_map/all_gather | solution.py:37
  343.2 10.2 convolution_convert_fusion.2
  353.4 0.0 all-gather.22.cloned.1.call-start
  353.4 0.5 all-gather.22.cloned.1.call-update
  354.0 0.2 all-gather.26.cloned.1.call-start
  354.2 122.0 %all-gather.24.cloned.1.call-done = bf16[4096,1024]{1,0:T(8,128)(2,1)} async-done(((bf16[512,1024]{1,0:T(8,128)(2,1)}), bf16[4096,1024]{1,0:T(8,128)(2,1)}) %all-gather.24.cloned.1.call-update) | async-done | bytes 8388624 | tf_op jit(solution)/shard_map/all_gather | solution.py:27
  476.2 10.9 fusion.2
  487.1 0.0 all-gather.26.cloned.1.call-update
  487.1 0.0 all-gather.30.cloned.1.call-start
  487.1 23.2 %all-gather.22.cloned.1.call-done = bf16[512,4096]{1,0:T(8,128)(2,1)} async-done(((bf16[512,1024]{1,0:T(8,128)(2,1)}), bf16[512,4096]{1,0:T(8,128)(2,1)}) %all-gather.22.cloned.1.call-update) | async-done | bytes 4194320 | tf_op jit(solution)/shard_map/all_gather | solution.py:34
  510.3 127.0 %all-gather.26.cloned.1.call-done = bf16[4096,1024]{0,1:T(8,128)(2,1)} async-done(((bf16[512,1024]{0,1:T(8,128)(2,1)}), bf16[4096,1024]{0,1:T(8,128)(2,1)}) %all-gather.26.cloned.1.call-update) | async-done | bytes 8388624 | tf_op jit(solution)/shard_map/all_gather | solution.py:37
  637.3 10.2 convolution_convert_fusion.1
  647.5 0.0 all-gather.30.cloned.1.call-update
  647.5 0.0 all-gather.28.cloned.1.call-start
  647.5 0.7 all-gather.28.cloned.1.call-update
  648.2 0.3 all-gather.32.cloned.1.call-start
  648.5 121.8 %all-gather.30.cloned.1.call-done = bf16[4096,1024]{1,0:T(8,128)(2,1)} async-done(((bf16[512,1024]{1,0:T(8,128)(2,1)}), bf16[4096,1024]{1,0:T(8,128)(2,1)}) %all-gather.30.cloned.1.call-update) | async-done | bytes 8388624 | tf_op jit(solution)/shard_map/all_gather | solution.py:27
  770.3 10.9 fusion.3
  781.2 0.0 all-gather.32.cloned.1.call-update
  781.2 0.0 all-gather.36.cloned.1.call-start
  781.2 23.3 %all-gather.28.cloned.1.call-done = bf16[512,4096]{1,0:T(8,128)(2,1)} async-done(((bf16[512,1024]{1,0:T(8,128)(2,1)}), bf16[512,4096]{1,0:T(8,128)(2,1)}) %all-gather.28.cloned.1.call-update) | async-done | bytes 4194320 | tf_op jit(solution)/shard_map/all_gather | solution.py:34
  804.5 126.9 %all-gather.32.cloned.1.call-done = bf16[4096,1024]{0,1:T(8,128)(2,1)} async-done(((bf16[512,1024]{0,1:T(8,128)(2,1)}), bf16[4096,1024]{0,1:T(8,128)(2,1)}) %all-gather.32.cloned.1.call-update) | async-done | bytes 8388624 | tf_op jit(solution)/shard_map/all_gather | solution.py:37
  931.4 10.2 convolution_convert_fusion
  941.6 0.0 all-gather.34.cloned.1.call-start
  941.6 0.5 all-gather.34.cloned.1.call-update
  942.2 0.3 all-gather.38.cloned.1.call-start
  942.5 121.9 %all-gather.36.cloned.1.call-done = bf16[4096,1024]{1,0:T(8,128)(2,1)} async-done(((bf16[512,1024]{1,0:T(8,128)(2,1)}), bf16[4096,1024]{1,0:T(8,128)(2,1)}) %all-gather.36.cloned.1.call-update) | async-done | bytes 8388624 | tf_op jit(solution)/shard_map/all_gather | solution.py:27
  1064.4 12.9 %multiply_reduce_fusion.3 = (f32[]{:T(128)}, f32[]{:T(128)}, f32[]{:T(128)}, f32[]{:T(128)}, bf16[512,1024]{0,1:T(8,128)(2,1)}) fusion(f32[1024,512]{1,0:T(8,128)S(1)} %get-tuple-element.10, s32[512]{0:T(512)S(1)} %iota_add_fusion.1, s32[1024]{0:T(1024)S(1)} %iota_add_fusion, f32[1024,512]{1,0:T(8,128)} %get-tuple-element.12, ...), kind=kOutput, calls=%fused_computation.17 | convolution fusion | flops 4303355904 | bytes 19929104 | tf_op jit(solution)/shard_map/dot_general | solution.py:25
  1077.4 2.6 pad_maximum_fusion
  1079.9 39.1 %psum.15 = f32[4]{0:T(128)S(1)} all-reduce(f32[4]{0:T(128)S(1)} %pad_maximum_fusion), channel_id=1, replica_groups=mesh['row'=8,'col'=4] {'row','col'}, use_global_device_ids=true, to_apply=%region_6.0 | all-reduce | flops 4 | bytes 32 | tf_op jit(solution)/shard_map/psum | solution.py:40
  1119.1 0.5 multiply_sqrt_fusion
  1119.6 107.3 %all-gather.38.cloned.1.call-done = bf16[4096,1024]{0,1:T(8,128)(2,1)} async-done(((bf16[512,1024]{0,1:T(8,128)(2,1)}), bf16[4096,1024]{0,1:T(8,128)(2,1)}) %all-gather.38.cloned.1.call-update) | async-done | bytes 8388624 | tf_op jit(solution)/shard_map/all_gather | solution.py:37
  1226.9 10.5 fusion.6
  (7 shorter events, 0.1 us)
Async XLA Ops:
  7.2 49.7 %all-gather.18.cloned.1.call-start = ((), (), s32[]{:S(2)}) async-start(), calls=%async_computation.2 | async-start | bytes 5242880 | tf_op jit(solution)/shard_map/all_gather | solution.py:20
  11.5 170.0 %all-gather.16.cloned.1.call-start = ((), (), s32[]{:S(2)}) async-start(), calls=%async_computation.1 | async-start | bytes 9437184 | tf_op jit(solution)/shard_map/all_gather | solution.py:27
  56.1 159.7 %all-gather.14.cloned.1.call-start = ((), (), s32[]{:S(2)}) async-start(), calls=%async_computation | async-start | bytes 5242880 | tf_op jit(solution)/shard_map/all_gather | solution.py:34
  56.8 286.4 %all-gather.20.cloned.1.call-start = ((), (), s32[]{:S(2)}) async-start(), calls=%async_computation.3 | async-start | bytes 9437184 | tf_op jit(solution)/shard_map/all_gather | solution.py:37
  191.6 284.6 %all-gather.24.cloned.1.call-start = ((), (), s32[]{:S(2)}) async-start(), calls=%async_computation.5 | async-start | bytes 9437184 | tf_op jit(solution)/shard_map/all_gather | solution.py:27
  353.4 156.9 %all-gather.22.cloned.1.call-start = ((), (), s32[]{:S(2)}) async-start(), calls=%async_computation.4 | async-start | bytes 5242880 | tf_op jit(solution)/shard_map/all_gather | solution.py:34
  354.0 283.3 %all-gather.26.cloned.1.call-start = ((), (), s32[]{:S(2)}) async-start(), calls=%async_computation.6 | async-start | bytes 9437184 | tf_op jit(solution)/shard_map/all_gather | solution.py:37
  487.1 283.2 %all-gather.30.cloned.1.call-start = ((), (), s32[]{:S(2)}) async-start(), calls=%async_computation.8 | async-start | bytes 9437184 | tf_op jit(solution)/shard_map/all_gather | solution.py:27
  647.5 157.0 %all-gather.28.cloned.1.call-start = ((), (), s32[]{:S(2)}) async-start(), calls=%async_computation.7 | async-start | bytes 5242880 | tf_op jit(solution)/shard_map/all_gather | solution.py:34
  648.2 283.2 %all-gather.32.cloned.1.call-start = ((), (), s32[]{:S(2)}) async-start(), calls=%async_computation.9 | async-start | bytes 9437184 | tf_op jit(solution)/shard_map/all_gather | solution.py:37
  781.2 283.2 %all-gather.36.cloned.1.call-start = ((), (), s32[]{:S(2)}) async-start(), calls=%async_computation.11 | async-start | bytes 9437184 | tf_op jit(solution)/shard_map/all_gather | solution.py:27
  941.6 178.0 %all-gather.34.cloned.1.call-start = ((), (), s32[]{:S(2)}) async-start(), calls=%async_computation.10 | async-start | bytes 5242880 | tf_op jit(solution)/shard_map/all_gather | solution.py:34
  942.2 284.7 %all-gather.38.cloned.1.call-start = ((), (), s32[]{:S(2)}) async-start(), calls=%async_computation.12 | async-start | bytes 9437184 | tf_op jit(solution)/shard_map/all_gather | solution.py:37
Sparse Core Ops, SparseCore 0:
  11.6 37.4 all-gather.17
  56.2 125.2 all-gather.15
  183.1 32.6 all-gather.13
  218.2 124.9 all-gather.19
  353.5 122.6 all-gather.23
  477.6 32.6 all-gather.21
  512.3 124.9 all-gather.25
  647.6 122.6 all-gather.29
  771.9 32.6 all-gather.27
  806.4 124.9 all-gather.31
  941.7 122.6 all-gather.35
  1065.8 33.3 all-gather.33
  1101.2 125.6 all-gather.37
where the time goes:
time: 1250 us; the launch traced here: 1240 us
  waiting for transfers between devices  1050 us (84%)
  matrix products  85.8 us (7%)
  blocking collectives  81.7 us (7%)
  between operations  15.1 us (1%)
    all_gather x4, waiting for transfers between devices, shards(): lax.all_gather(cur_low, 'row', axis=0, tiled=True)  490 us
    all_gather x4, waiting for transfers between devices, shards(): lax.all_gather(shift_low, 'row', axis=0, tiled=True)  489 us
    all_gather x4, waiting for transfers between devices, shards(): iterate_rows = lax.all_gather(cur_low, 'col', axis=1, tiled=True)  70.5 us
    dot_general x4, matrix products, shards(): jnp.dot(panel_rows, lax.all_gather(cur_low, 'row', axis=0, tiled=True), p...  44.8 us
    psum x1, blocking collectives, shards(): sq_total = lax.psum(jnp.sum(matrix * matrix), ('row', 'col'))  42.5 us
    dot_general x4, matrix products, shards(): jnp.dot(iterate_rows, lax.all_gather(shift_low, 'row', axis=0, tiled=True...  41 us
    psum x1, blocking collectives, shards(): summed = lax.psum(jnp.stack(partial_list), ('row', 'col'))  39.1 us
  transfers between devices with their start and end apart: 13, of which 11 were waited for; matrix products, arithmetic and copies ran while one was open for 4% of the time, Pallas kernels for 0%

commit v1 on v0

v1 whole, which is shorter than its diff:
```python
import jax
import jax.numpy as jnp
from jax import lax
from jax.sharding import PartitionSpec as P

ITERS = 4


def rounded(value):
    return lax.reduce_precision(value, 8, 7)


def first_iterate(panel, scale_low, row_start, col_start):
    rows = row_start + lax.broadcasted_iota(jnp.int32, panel.shape, 0)
    cols = col_start + lax.broadcasted_iota(jnp.int32, panel.shape, 1)
    eye = (rows == cols).astype(jnp.float32)
    shift = rounded(eye + (eye - scale_low * panel.astype(jnp.float32)))
    return (scale_low * shift).astype(jnp.bfloat16)


def transpose_blocks(block, row_size, col_size):
    ratio = row_size // col_size
    side = block.shape[0]
    row_index = lax.axis_index("row")
    pieces = []
    for turn in range(ratio):
        pairs = []
        for row in range(row_size):
            for col in range(col_size):
                target_row = ratio * col + (row + turn) % ratio
                pairs.append((row * col_size + col, target_row * col_size + row // ratio))
        half = lax.rem(row_index + turn, ratio)
        piece = lax.dynamic_slice_in_dim(block, half * side, side, axis=1)
        pieces.append(lax.ppermute(piece, ("row", "col"), pairs).T)
    out = jnp.zeros_like(block)
    for turn in range(ratio):
        half = lax.rem(row_index - turn + ratio, ratio)
        out = lax.dynamic_update_slice_in_dim(out, pieces[turn], half * side, axis=1)
    return out


def shards(matrix):
    row_count, col_count = matrix.shape
    row_size, col_size = lax.axis_size("row"), lax.axis_size("col")
    order = col_count * col_size
    row_start = lax.axis_index("row") * row_count
    col_start = lax.axis_index("col") * col_count
    global_rows = row_start + lax.broadcasted_iota(jnp.int32, (row_count, col_count), 0)
    global_cols = col_start + lax.broadcasted_iota(jnp.int32, (row_count, col_count), 1)
    eye_block = (global_rows == global_cols).astype(jnp.float32)
    mat_low = matrix.astype(jnp.bfloat16)
    sq_total = lax.psum(jnp.sum(matrix * matrix), ("row", "col"))
    panel_rows = lax.all_gather(mat_low, "col", axis=1, tiled=True)
    panel_cols = lax.all_gather(mat_low, "row", axis=0, tiled=True)
    start_scale = jnp.sqrt(jnp.float32(order)) / jnp.sqrt(sq_total)
    scale_low = rounded(start_scale)
    residual = eye_block - scale_low * rounded(matrix)
    partial_list = [jnp.sum(residual * residual)]
    iterate_rows = first_iterate(panel_rows, scale_low, row_start, 0)
    iterate_cols = first_iterate(panel_cols, scale_low, 0, col_start)
    for iteration in range(1, ITERS):
        product = jnp.dot(iterate_rows, panel_cols, preferred_element_type=jnp.float32)
        residual = eye_block - product
        partial_list.append(jnp.sum(residual * residual))
        shift_low = (eye_block + residual).astype(jnp.bfloat16)
        current = jnp.dot(
            lax.all_gather(shift_low, "col", axis=1, tiled=True),
            iterate_cols,
            preferred_element_type=jnp.float32,
        )
        if iteration < ITERS - 1:
            cur_low = current.astype(jnp.bfloat16)
            iterate_rows = lax.all_gather(cur_low, "col", axis=1, tiled=True)
            iterate_cols = lax.all_gather(cur_low, "row", axis=0, tiled=True)
    summed = lax.psum(jnp.stack(partial_list), ("row", "col"))
    residual_norms = jnp.sqrt(summed / order)
    return (transpose_blocks(current, row_size, col_size), residual_norms)


def solution(mesh):
    in_specs = (P("row", "col"),)
    out_specs = (P("row", "col"), P())
    return jax.shard_map(shards, mesh=mesh, in_specs=in_specs, out_specs=out_specs, check_vma=False)
```

time: 1250 us -> 791 us (0.63)
  waiting for transfers between devices: 1050 us -> 543 us
  blocking collectives: 81.7 us -> 152 us
  matrix products: 85.8 us -> 66.4 us
    all_gather x8 -> x6, waiting for transfers between devices: 979 us -> 474 us  [the longest x2 253 us: shards(): iterate_cols = lax.all_gather(cur_low, 'row', axis=0, tiled=True)]
    psum x1, blocking collectives: 39.1 us -> 110 us  [shards(): summed = lax.psum(jnp.stack(partial_list), ('row', 'col'))]
    dot_general x8 -> x6, matrix products: 85.8 us -> 66.4 us  [the longest x3 36.2 us: shards(): jnp.dot(iterate_rows, panel_cols, preferred_element_type=jnp.float32)]
    all_gather x4 -> x2, waiting for transfers between devices: 70.5 us -> 67.1 us  [shards(): iterate_rows = lax.all_gather(cur_low, 'col', axis=1, tiled=True)]
  transfers between devices with their start and end apart: 13 -> 11, of which waited for: 11 -> 8; matrix products, arithmetic and copies ran while one was open for 4% -> 1% of each run, Pallas kernels for 0% -> 0%
where the time goes in v1:
time: 791 us
  waiting for transfers between devices  543 us (69%)
  blocking collectives  152 us (19%)
  matrix products  66.4 us (8%)
  between operations  15.1 us (2%)
    all_gather x2, waiting for transfers between devices, shards(): iterate_cols = lax.all_gather(cur_low, 'row', axis=0, tiled=True)  253 us
    all_gather x1, waiting for transfers between devices, shards(): panel_cols = lax.all_gather(mat_low, 'row', axis=0, tiled=True)  120 us
    psum x1, blocking collectives, shards(): summed = lax.psum(jnp.stack(partial_list), ('row', 'col'))  110 us
    all_gather x3, waiting for transfers between devices, shards(): lax.all_gather(shift_low, 'col', axis=1, tiled=True)  101 us
    all_gather x2, waiting for transfers between devices, shards(): iterate_rows = lax.all_gather(cur_low, 'col', axis=1, tiled=True)  67.1 us
    psum x1, blocking collectives, shards(): sq_total = lax.psum(jnp.sum(matrix * matrix), ('row', 'col'))  42.5 us
    dot_general x3, matrix products, shards(): jnp.dot(iterate_rows, panel_cols, preferred_element_type=jnp.float32)  36.2 us
    dot_general x3, matrix products, shards(): jnp.dot(lax.all_gather(shift_low, 'col', axis=1, tiled=True), iterate_col...  30.3 us
  transfers between devices with their start and end apart: 11, of which 8 were waited for; matrix products, arithmetic and copies ran while one was open for 1% of the time, Pallas kernels for 0%

profile of v1, /device:TPU:0, one launch (start us, length us, event | category | flops | bytes accessed | tf_op | source)
XLA Modules:
  0.0 790.7 jit_solution(10998236796299218012)
XLA Ops:
  7.2 0.0 all-gather.10.cloned.1.call-start
  7.2 4.3 multiply_reduce_fusion.3
  11.5 0.0 all-gather.10.cloned.1.call-update
  11.5 0.0 all-gather.12.cloned.1.call-start
  11.5 0.7 all-gather.12.cloned.1.call-update
  12.3 0.0 all-gather.14.cloned.1.call-start
  12.3 42.5 %psum.14 = f32[]{:T(128)} all-reduce(f32[]{:T(128)} %get-tuple-element.9), channel_id=1, replica_groups=mesh['row'=8,'col'=4] {'row','col'}, use_global_device_ids=true, to_apply=%region_1.0 | all-reduce | flops 1 | bytes 8 | tf_op jit(solution)/shard_map/psum | solution.py:52
  56.0 120.3 %all-gather.12.cloned.1.call-done = bf16[4096,1024]{1,0:T(8,128)(2,1)} async-done(((bf16[512,1024]{1,0:T(8,128)(2,1)}), bf16[4096,1024]{1,0:T(8,128)(2,1)}) %all-gather.12.cloned.1.call-update) | async-done | bytes 8388624 | tf_op jit(solution)/shard_map/all_gather | solution.py:54
  176.3 12.1 %fusion.12 = (bf16[512,1024]{1,0:T(8,128)(2,1)}, f32[512,1024]{1,0:T(8,128)}) fusion(s32[1024]{0:T(1024)S(1)} %iota_add_fusion, s32[512]{0:T(512)S(1)} %iota_add_fusion.1, bf16[4096,1024]{1,0:T(8,128)(2,1)} %all-gather.12.cloned.1.call-done, bf16[512,4096]{1,0:T(8,128)(2,1)} %all-gather.10.cloned.1.call-done, f32[]{:T(128)} %reduce_precision.12), kind=kOutput, calls=%fused_computation.21 | convolution fusion | flops 4316463104 | bytes 15734788 | tf_op jit(solution)/shard_map/dot_general | solution.py:62
  188.4 0.0 all-gather.14.cloned.1.call-update
  188.5 0.0 all-gather.16.cloned.1.call-start
  188.5 32.7 %all-gather.14.cloned.1.call-done = bf16[512,4096]{1,0:T(8,128)(2,1)} async-done(((bf16[512,1024]{1,0:T(8,128)(2,1)}), bf16[512,4096]{1,0:T(8,128)(2,1)}) %all-gather.14.cloned.1.call-update) | async-done | bytes 4194320 | tf_op jit(solution)/shard_map/all_gather | solution.py:67
  221.3 12.0 %fusion.17 = bf16[512,1024]{1,0:T(8,128)(2,1)} fusion(bf16[512,4096]{1,0:T(8,128)(2,1)} %all-gather.14.cloned.1.call-done, bf16[4096,1024]{1,0:T(8,128)(2,1)} %all-gather.12.cloned.1.call-done, s32[1024]{0:T(1024)S(1)} %iota_add_fusion, f32[]{:T(128)} %reduce_precision.12), kind=kOutput, calls=%fused_computation.30 | convolution fusion | flops 4333240320 | bytes 13635588 | tf_op jit(solution)/shard_map/dot_general | solution.py:66
  233.2 0.0 all-gather.16.cloned.1.call-update
  233.3 0.2 all-gather.18.cloned.1.call-start
  233.5 34.4 %all-gather.16.cloned.1.call-done = bf16[512,4096]{1,0:T(8,128)(2,1)} async-done(((bf16[512,1024]{1,0:T(8,128)(2,1)}), bf16[512,4096]{1,0:T(8,128)(2,1)}) %all-gather.16.cloned.1.call-update) | async-done | bytes 4194320 | tf_op jit(solution)/shard_map/all_gather | solution.py:73
  267.9 10.9 %fusion.13 = (bf16[512,1024]{1,0:T(8,128)(2,1)}, f32[512,1024]{1,0:T(8,128)}) fusion(s32[1024]{0:T(1024)S(1)} %iota_add_fusion, s32[512]{0:T(512)S(1)} %iota_add_fusion.1, bf16[512,4096]{1,0:T(8,128)(2,1)} %all-gather.16.cloned.1.call-done, bf16[4096,1024]{1,0:T(8,128)(2,1)} %all-gather.12.cloned.1.call-done), kind=kOutput, calls=%fused_computation.22 | convolution fusion | flops 4297588736 | bytes 15734784 | tf_op jit(solution)/shard_map/dot_general | solution.py:62
  278.7 0.0 all-gather.18.cloned.1.call-update
  278.8 0.0 all-gather.20.cloned.1.call-start
  278.8 0.5 all-gather.20.cloned.1.call-update
  279.3 0.0 copy-start.1
  279.4 0.0 all-gather.22.cloned.1.call-start
  279.4 34.0 %all-gather.18.cloned.1.call-done = bf16[512,4096]{1,0:T(8,128)(2,1)} async-done(((bf16[512,1024]{1,0:T(8,128)(2,1)}), bf16[512,4096]{1,0:T(8,128)(2,1)}) %all-gather.18.cloned.1.call-update) | async-done | bytes 4194320 | tf_op jit(solution)/shard_map/all_gather | solution.py:67
  313.4 126.5 %all-gather.20.cloned.1.call-done = bf16[4096,1024]{1,0:T(8,128)(2,1)} async-done(((bf16[512,1024]{1,0:T(8,128)(2,1)}), bf16[4096,1024]{1,0:T(8,128)(2,1)}) %all-gather.20.cloned.1.call-update) | async-done | bytes 8388624 | tf_op jit(solution)/shard_map/all_gather | solution.py:74
  439.9 10.2 %convolution_convert_fusion = bf16[512,1024]{1,0:T(8,128)(2,1)} fusion(bf16[512,4096]{1,0:T(8,128)(2,1)} %all-gather.18.cloned.1.call-done, bf16[4096,1024]{1,0:T(8,128)(2,1)} %all-gather.20.cloned.1.call-done), kind=kOutput, calls=%fused_computation.31 | convolution fusion | flops 4295491584 | bytes 13631488 | tf_op jit(solution)/shard_map/dot_general | solution.py:66
  450.0 0.0 all-gather.22.cloned.1.call-update
  450.1 0.0 all-gather.24.cloned.1.call-start
  450.1 32.7 %all-gather.22.cloned.1.call-done = bf16[512,4096]{1,0:T(8,128)(2,1)} async-done(((bf16[512,1024]{1,0:T(8,128)(2,1)}), bf16[512,4096]{1,0:T(8,128)(2,1)}) %all-gather.22.cloned.1.call-update) | async-done | bytes 4194320 | tf_op jit(solution)/shard_map/all_gather | solution.py:73
  482.8 13.2 %fusion.16 = (f32[]{:T(128)}, f32[]{:T(128)}, f32[]{:T(128)}, f32[]{:T(128)}, bf16[512,1024]{1,0:T(8,128)(2,1)}) fusion(f32[512,1024]{1,0:T(8,128)S(1)} %copy-done.1, f32[]{:T(128)} %reduce_precision.12, s32[1024]{0:T(1024)S(1)} %iota_add_fusion, s32[512]{0:T(512)S(1)} %iota_add_fusion.1, f32[512,1024]{1,0:T(8,128)} %get-tuple-element.14, ...), kind=kOutput, calls=%fused_computation.25 | convolution fusion | flops 4304404480 | bytes 19929108 | tf_op jit(solution)/shard_map/dot_general | solution.py:62
  496.0 0.0 all-gather.24.cloned.1.call-update
  496.0 0.3 all-gather.26.cloned.1.call-start
  496.3 0.5 all-gather.26.cloned.1.call-update
  496.8 33.9 %all-gather.24.cloned.1.call-done = bf16[512,4096]{1,0:T(8,128)(2,1)} async-done(((bf16[512,1024]{1,0:T(8,128)(2,1)}), bf16[512,4096]{1,0:T(8,128)(2,1)}) %all-gather.24.cloned.1.call-update) | async-done | bytes 4194320 | tf_op jit(solution)/shard_map/all_gather | solution.py:67
  530.6 126.6 %all-gather.26.cloned.1.call-done = bf16[4096,1024]{1,0:T(8,128)(2,1)} async-done(((bf16[512,1024]{1,0:T(8,128)(2,1)}), bf16[4096,1024]{1,0:T(8,128)(2,1)}) %all-gather.26.cloned.1.call-update) | async-done | bytes 8388624 | tf_op jit(solution)/shard_map/all_gather | solution.py:74
  657.3 8.1 %fusion.20 = f32[512,1024]{1,0:T(8,128)S(1)} fusion(bf16[512,4096]{1,0:T(8,128)(2,1)} %all-gather.24.cloned.1.call-done, bf16[4096,1024]{1,0:T(8,128)(2,1)} %all-gather.26.cloned.1.call-done), kind=kOutput, calls=%fused_computation.40 | convolution fusion | flops 4294967296 | bytes 14680064 | tf_op jit(solution)/shard_map/dot_general | solution.py:66
  665.4 0.2 constant_dynamic-slice_fusion
  665.7 1.6 collective-permute-start
  667.3 0.6 collective-permute-start.1
  667.8 2.5 pad_maximum_fusion
  670.4 109.5 %psum.15 = f32[4]{0:T(128)S(1)} all-reduce(f32[4]{0:T(128)S(1)} %pad_maximum_fusion), channel_id=1, replica_groups=mesh['row'=8,'col'=4] {'row','col'}, use_global_device_ids=true, to_apply=%region_6.0 | all-reduce | flops 4 | bytes 32 | tf_op jit(solution)/shard_map/psum | solution.py:75
  779.9 0.5 multiply_sqrt_fusion
  780.4 1.6 copy.3
  782.0 0.3 copy.4
  782.4 0.2 broadcast_in_dim.3
  782.6 0.1 constant_dynamic-update-slice_fusion.1
  782.7 0.1 constant_dynamic-update-slice_fusion
  782.8 0.0 copy-start
  782.8 1.3 copy-done
  (6 shorter events, 0.0 us)
Async XLA Ops:
  7.2 48.9 %all-gather.10.cloned.1.call-start = ((), (), s32[]{:S(2)}) async-start(), calls=%async_computation | async-start | bytes 5242880 | tf_op jit(solution)/shard_map/all_gather | solution.py:53
  11.5 164.8 %all-gather.12.cloned.1.call-start = ((), (), s32[]{:S(2)}) async-start(), calls=%async_computation.1 | async-start | bytes 9437184 | tf_op jit(solution)/shard_map/all_gather | solution.py:54
  12.3 209.0 %all-gather.14.cloned.1.call-start = ((), (), s32[]{:S(2)}) async-start(), calls=%async_computation.2 | async-start | bytes 5242880 | tf_op jit(solution)/shard_map/all_gather | solution.py:67
  188.5 79.4 %all-gather.16.cloned.1.call-start = ((), (), s32[]{:S(2)}) async-start(), calls=%async_computation.3 | async-start | bytes 5242880 | tf_op jit(solution)/shard_map/all_gather | solution.py:73
  233.3 80.1 %all-gather.18.cloned.1.call-start = ((), (), s32[]{:S(2)}) async-start(), calls=%async_computation.4 | async-start | bytes 5242880 | tf_op jit(solution)/shard_map/all_gather | solution.py:67
  278.8 161.1 %all-gather.20.cloned.1.call-start = ((), (), s32[]{:S(2)}) async-start(), calls=%async_computation.5 | async-start | bytes 9437184 | tf_op jit(solution)/shard_map/all_gather | solution.py:74
  279.3 203.5 %copy-start.1 = (f32[512,1024]{1,0:T(8,128)S(1)}, f32[512,1024]{1,0:T(8,128)}, u32[]{:S(2)}) copy-start(f32[512,1024]{1,0:T(8,128)} %param.1) | copy-start | bytes 6291460
  279.4 203.5 %all-gather.22.cloned.1.call-start = ((), (), s32[]{:S(2)}) async-start(), calls=%async_computation.6 | async-start | bytes 5242880 | tf_op jit(solution)/shard_map/all_gather | solution.py:73
  450.1 80.6 %all-gather.24.cloned.1.call-start = ((), (), s32[]{:S(2)}) async-start(), calls=%async_computation.7 | async-start | bytes 5242880 | tf_op jit(solution)/shard_map/all_gather | solution.py:67
  496.0 161.3 %all-gather.26.cloned.1.call-start = ((), (), s32[]{:S(2)}) async-start(), calls=%async_computation.8 | async-start | bytes 9437184 | tf_op jit(solution)/shard_map/all_gather | solution.py:74
  665.7 114.8 %collective-permute-start = (f32[512,512]{1,0:T(8,128)S(1)}, f32[512,512]{1,0:T(8,128)}, u32[]{:S(2)}, u32[]{:S(2)}) collective-permute-start(f32[512,512]{1,0:T(8,128)S(1)} %get-tuple-element.8), channel_id=1, source_target_pairs={{0,0},{1,8},{2,16},{3,24},{4,4},{5,12},{6,20},{7,28},{8,1},{9,9},{... | collective-permute-start | bytes 3145736 | tf_op jit(solution)/shard_map/ppermute | solution.py:34
  667.3 114.7 %collective-permute-start.1 = (f32[512,512]{1,0:T(8,128)S(1)}, f32[512,512]{1,0:T(8,128)S(1)}, u32[]{:S(2)}, u32[]{:S(2)}) collective-permute-start(f32[512,512]{1,0:T(8,128)S(1)} %get-tuple-element.7), channel_id=1, source_target_pairs={{0,4},{1,12},{2,20},{3,28},{4,0},{5,8},{6,16},{7,24},{8,5},{9,13},... | collective-permute-start | bytes 3145736 | tf_op jit(solution)/shard_map/ppermute | solution.py:34
  782.8 1.3 copy-start
Sparse Core Ops, SparseCore 0:
  11.6 37.4 all-gather.9
  51.8 124.4 all-gather.11
  188.6 32.6 all-gather.13
  233.4 34.4 all-gather.15
  278.9 34.4 all-gather.17
  315.4 124.4 all-gather.19
  450.2 32.6 all-gather.21
  496.1 34.4 all-gather.23
  532.8 124.4 all-gather.25

commit v2 on v1

--- a/solution.py
+++ b/solution.py
@@ -39,6 +39,21 @@
     return out
 
 
+def gather_cols(block, col_size):
+    width = block.shape[1]
+    col_index = lax.axis_index("col")
+    panel = jnp.zeros((block.shape[0], width * col_size), block.dtype)
+    panel = lax.dynamic_update_slice_in_dim(panel, block, col_index * width, axis=1)
+    moved = []
+    for turn in range(1, col_size):
+        pairs = [(col, (col + turn) % col_size) for col in range(col_size)]
+        moved.append(lax.ppermute(block, "col", pairs))
+    for turn in range(1, col_size):
+        owner = lax.rem(col_index - turn + col_size, col_size)
+        panel = lax.dynamic_update_slice_in_dim(panel, moved[turn - 1], owner * width, axis=1)
+    return panel
+
+
 def shards(matrix):
     row_count, col_count = matrix.shape
     row_size, col_size = lax.axis_size("row"), lax.axis_size("col")
@@ -50,7 +65,7 @@
     eye_block = (global_rows == global_cols).astype(jnp.float32)
     mat_low = matrix.astype(jnp.bfloat16)
     sq_total = lax.psum(jnp.sum(matrix * matrix), ("row", "col"))
-    panel_rows = lax.all_gather(mat_low, "col", axis=1, tiled=True)
+    panel_rows = gather_cols(mat_low, col_size)
     panel_cols = lax.all_gather(mat_low, "row", axis=0, tiled=True)
     start_scale = jnp.sqrt(jnp.float32(order)) / jnp.sqrt(sq_total)
     scale_low = rounded(start_scale)
@@ -64,14 +79,14 @@
         partial_list.append(jnp.sum(residual * residual))
         shift_low = (eye_block + residual).astype(jnp.bfloat16)
         current = jnp.dot(
-            lax.all_gather(shift_low, "col", axis=1, tiled=True),
+            gather_cols(shift_low, col_size),
             iterate_cols,
             preferred_element_type=jnp.float32,
         )
         if iteration < ITERS - 1:
             cur_low = current.astype(jnp.bfloat16)
-            iterate_rows = lax.all_gather(cur_low, "col", axis=1, tiled=True)
             iterate_cols = lax.all_gather(cur_low, "row", axis=0, tiled=True)
+            iterate_rows = gather_cols(cur_low, col_size)
     summed = lax.psum(jnp.stack(partial_list), ("row", "col"))
     residual_norms = jnp.sqrt(summed / order)
     return (transpose_blocks(current, row_size, col_size), residual_norms)

time: 791 us -> 606 us (0.77)
  waiting for transfers between devices: 543 us -> 269 us
  local copies, waits for them, and re-layouts: 3.86 us -> 42.7 us
  blocking collectives: 152 us -> 179 us
  starting transfers between devices: 2.96 us -> 28.2 us
    all_gather x2, waiting for transfers between devices: 253 us -> 26.5 us  [shards(): iterate_cols = lax.all_gather(cur_low, 'row', axis=0, tiled=True)]
    ppermute x0 -> x18, waiting for transfers between devices: none -> 209 us  [gather_cols(): moved.append(lax.ppermute(block, 'col', pairs))]
    all_gather x6 -> x0, waiting for transfers between devices: 168 us -> none  [the longest x3 101 us: shards(): lax.all_gather(shift_low, 'col', axis=1, tiled=True)]
    all_gather x1, waiting for transfers between devices: 120 us -> 33 us  [shards(): panel_cols = lax.all_gather(mat_low, 'row', axis=0, tiled=True)]
    psum x1, blocking collectives: 42.5 us -> 82.5 us  [shards(): sq_total = lax.psum(jnp.sum(matrix * matrix), ('row', 'col'))]
    dynamic_update_slice x0 -> x18, local copies, waits for them, and re-layouts: none -> 22 us  [gather_cols(): lax.dynamic_update_slice_in_dim(panel, moved[turn - 1], owner * width, ax...]
    ppermute x0 -> x18, starting transfers between devices: none -> 18 us  [gather_cols(): moved.append(lax.ppermute(block, 'col', pairs))]
    psum x1, blocking collectives: 110 us -> 96.7 us  [shards(): summed = lax.psum(jnp.stack(partial_list), ('row', 'col'))]
  transfers between devices with their start and end apart: 11 -> 23, of which waited for: 8 -> 18; matrix products, arithmetic and copies ran while one was open for 1% -> 10% of each run, Pallas kernels for 0% -> 0%
where the time goes in v2:
time: 606 us; the launch traced here: 605 us
  waiting for transfers between devices  269 us (44%)
  blocking collectives  179 us (30%)
  matrix products  59.7 us (10%)
  local copies, waits for them, and re-layouts  42.7 us (7%)
  starting transfers between devices  28.2 us (5%)
  between operations  15.1 us (2%)
  other arithmetic  11.2 us (2%)
    ppermute x18, waiting for transfers between devices, gather_cols(): moved.append(lax.ppermute(block, 'col', pairs))  209 us
    psum x1, blocking collectives, shards(): summed = lax.psum(jnp.stack(partial_list), ('row', 'col'))  96.7 us
    psum x1, blocking collectives, shards(): sq_total = lax.psum(jnp.sum(matrix * matrix), ('row', 'col'))  82.5 us
    dot_general x3, matrix products, shards(): jnp.dot(iterate_rows, panel_cols, preferred_element_type=jnp.float32)  33.8 us
    all_gather x1, waiting for transfers between devices, shards(): panel_cols = lax.all_gather(mat_low, 'row', axis=0, tiled=True)  33 us
    all_gather x2, waiting for transfers between devices, shards(): iterate_cols = lax.all_gather(cur_low, 'row', axis=0, tiled=True)  26.5 us
    dot_general x3, matrix products, shards(): jnp.dot(gather_cols(shift_low, col_size), iterate_cols, preferred_element...  26 us
    dynamic_update_slice x18, local copies, waits for them, and re-layouts, gather_cols(): lax.dynamic_update_slice_in_dim(panel, moved[turn - 1], owner * width, ax...  22 us
  transfers between devices with their start and end apart: 23, of which 18 were waited for; matrix products, arithmetic and copies ran while one was open for 10% of the time, Pallas kernels for 0%

profile of v2, /device:TPU:0, one launch (start us, length us, event | category | flops | bytes accessed | tf_op | source)
XLA Modules:
  0.0 604.7 jit_solution(13643633760991632931)
XLA Ops:
  7.2 2.5 broadcast.22.clone.4
  9.7 1.7 constant_dynamic-update-slice_fusion.25
  12.0 2.6 collective-permute-start.1
  14.6 1.4 collective-permute-start.2
  17.1 82.5 %psum.14 = f32[]{:T(128)} all-reduce(f32[]{:T(128)} %multiply_reduce_fusion.3), channel_id=1, replica_groups=mesh['row'=8,'col'=4] {'row','col'}, use_global_device_ids=true, to_apply=%region_1.0 | all-reduce | flops 1 | bytes 8 | tf_op jit(solution)/shard_map/psum | solution.py:67
  100.8 2.4 constant_dynamic-update-slice_fusion.24
  103.2 2.3 constant_dynamic-update-slice_fusion.23
  106.6 33.0 %all-gather.4.cloned.1.call-done = bf16[4096,1024]{1,0:T(8,128)(2,1)} async-done(((bf16[512,1024]{1,0:T(8,128)(2,1)}), bf16[4096,1024]{1,0:T(8,128)(2,1)}) %all-gather.4.cloned.1.call-update) | async-done | bytes 8388624 | tf_op jit(solution)/shard_map/all_gather | solution.py:69
  140.2 12.6 %constant_dynamic-update-slice_fusion.21 = (bf16[512,4096]{1,0:T(8,128)(2,1)S(1)}, bf16[512,1024]{1,0:T(8,128)(2,1)S(1)}, f32[512,1024]{1,0:T(8,128)}) fusion(bf16[512,4096]{1,0:T(8,128)(2,1)S(1)} %broadcast.22.clone.3, s32[]{:T(128)S(6)} %select_n.14, s32[1024]{0:T(1024)S(1)} %iota_add_fusion, s32[512]{0:T(512)S(1)} %iota_add_fusion.1, ...), kind=kOutput, calls=%fused_computation.55 | convolution fusion | flops 4316463104 | bytes 16785416 | tf_op jit(solution)/shard_map/dot_general | solution.py:77
  152.8 1.4 collective-permute-start.4
  154.2 1.5 collective-permute-start.5
  155.7 22.0 %collective-permute-done.3 = bf16[512,1024]{1,0:T(8,128)(2,1)S(1)} collective-permute-done((bf16[512,1024]{1,0:T(8,128)(2,1)S(1)}, bf16[512,1024]{1,0:T(8,128)(2,1)S(1)}, u32[]{:S(2)}, u32[]{:S(2)}) %collective-permute-start.3) | collective-permute-done | bytes 1048608 | tf_op jit(solution)/shard_map/ppermute | solution.py:50
  179.0 20.7 %collective-permute-done.5 = bf16[512,1024]{1,0:T(8,128)(2,1)S(1)} collective-permute-done((bf16[512,1024]{1,0:T(8,128)(2,1)S(1)}, bf16[512,1024]{1,0:T(8,128)(2,1)S(1)}, u32[]{:S(2)}, u32[]{:S(2)}) %collective-permute-start.5) | collective-permute-done | bytes 1048608 | tf_op jit(solution)/shard_map/ppermute | solution.py:50
  200.3 7.3 %constant_dynamic-update-slice_fusion.17 = (bf16[512,4096]{1,0:T(8,128)(2,1)S(1)}, bf16[512,1024]{1,0:T(8,128)(2,1)}) fusion(bf16[512,4096]{1,0:T(8,128)(2,1)S(1)} %broadcast.22.clone.2, s32[]{:T(128)S(6)} %select_n.14, bf16[512,4096]{1,0:T(8,128)(2,1)S(1)} %constant_dynamic-update-slice_fusion.18, bf16[4096,1024]{1,0:T(8,128)(2,1)S(1)} %bitcast.17, ...), kind=kOutput, calls=%fused_computation.51 | convolution fusion | flops 4333240320 | bytes 14684168 | tf_op jit(solution)/shard_map/dot_general | solution.py:81
  207.6 2.0 copy-done.1
  210.6 1.4 collective-permute-start.7
  212.1 22.1 %collective-permute-done.6 = bf16[512,1024]{1,0:T(8,128)(2,1)S(1)} collective-permute-done((bf16[512,1024]{1,0:T(8,128)(2,1)}, bf16[512,1024]{1,0:T(8,128)(2,1)S(1)}, u32[]{:S(2)}, u32[]{:S(2)}) %collective-permute-start.6) | collective-permute-done | bytes 1048608 | tf_op jit(solution)/shard_map/ppermute | solution.py:50
  235.4 1.5 collective-permute-done.7
  238.0 18.2 %collective-permute-done.8 = bf16[512,1024]{1,0:T(8,128)(2,1)S(1)} collective-permute-done((bf16[512,1024]{1,0:T(8,128)(2,1)}, bf16[512,1024]{1,0:T(8,128)(2,1)S(1)}, u32[]{:S(2)}, u32[]{:S(2)}) %collective-permute-start.8) | collective-permute-done | bytes 1048608 | tf_op jit(solution)/shard_map/ppermute | solution.py:50
  257.4 2.7 broadcast.22.clone.1
  261.3 9.8 %constant_dynamic-update-slice_fusion.13 = (bf16[512,4096]{1,0:T(8,128)(2,1)}, bf16[512,1024]{1,0:T(8,128)(2,1)S(1)}, f32[512,1024]{1,0:T(8,128)}) fusion(bf16[512,4096]{1,0:T(8,128)(2,1)} %broadcast.22.clone.1, s32[]{:T(128)S(6)} %select_n.14, s32[1024]{0:T(1024)S(1)} %iota_add_fusion, s32[512]{0:T(512)S(1)} %iota_add_fusion.1, ...), kind=kOutput, calls=%fused_computation.47 | convolution fusion | flops 4297588736 | bytes 16783364 | tf_op jit(solution)/shard_map/dot_general | solution.py:77
  271.1 1.6 collective-permute-start.9
  274.1 20.3 %collective-permute-done.9 = bf16[512,1024]{1,0:T(8,128)(2,1)S(1)} collective-permute-done((bf16[512,1024]{1,0:T(8,128)(2,1)S(1)}, bf16[512,1024]{1,0:T(8,128)(2,1)S(1)}, u32[]{:S(2)}, u32[]{:S(2)}) %collective-permute-start.9) | collective-permute-done | bytes 1048608 | tf_op jit(solution)/shard_map/ppermute | solution.py:50
  295.5 3.2 collective-permute-done.10
  299.8 18.3 %collective-permute-done.11 = bf16[512,1024]{1,0:T(8,128)(2,1)S(1)} collective-permute-done((bf16[512,1024]{1,0:T(8,128)(2,1)S(1)}, bf16[512,1024]{1,0:T(8,128)(2,1)S(1)}, u32[]{:S(2)}, u32[]{:S(2)}) %collective-permute-start.11) | collective-permute-done | bytes 1048608 | tf_op jit(solution)/shard_map/ppermute | solution.py:50
  319.1 13.8 %all-gather.6.cloned.1.call-done = bf16[4096,1024]{1,0:T(8,128)(2,1)} async-done(((bf16[512,1024]{1,0:T(8,128)(2,1)}), bf16[4096,1024]{1,0:T(8,128)(2,1)}) %all-gather.6.cloned.1.call-update) | async-done | bytes 8388624 | tf_op jit(solution)/shard_map/all_gather | solution.py:88
  333.0 2.5 broadcast.22.clone
  335.5 10.6 %constant_dynamic-update-slice_fusion.9 = (bf16[512,4096]{1,0:T(8,128)(2,1)}, bf16[512,1024]{1,0:T(8,128)(2,1)}) fusion(bf16[512,4096]{1,0:T(8,128)(2,1)} %broadcast.22.clone, s32[]{:T(128)S(6)} %select_n.14, bf16[512,4096]{1,0:T(8,128)(2,1)} %constant_dynamic-update-slice_fusion.10, bf16[4096,1024]{1,0:T(8,128)(2,1)} %all-gather.6.cloned.1.call-done), kind=kOutput, calls=%fused_computation.43 | convolution fusion | flops 4295491584 | bytes 14680068 | tf_op jit(solution)/shard_map/dot_general | solution.py:81
  346.1 1.6 collective-permute-start.13
  347.7 1.4 collective-permute-start.14
  349.1 22.0 %collective-permute-done.12 = bf16[512,1024]{1,0:T(8,128)(2,1)S(1)} collective-permute-done((bf16[512,1024]{1,0:T(8,128)(2,1)}, bf16[512,1024]{1,0:T(8,128)(2,1)S(1)}, u32[]{:S(2)}, u32[]{:S(2)}) %collective-permute-start.12) | collective-permute-done | bytes 1048608 | tf_op jit(solution)/shard_map/ppermute | solution.py:50
  373.6 19.8 %collective-permute-done.14 = bf16[512,1024]{1,0:T(8,128)(2,1)S(1)} collective-permute-done((bf16[512,1024]{1,0:T(8,128)(2,1)}, bf16[512,1024]{1,0:T(8,128)(2,1)S(1)}, u32[]{:S(2)}, u32[]{:S(2)}) %collective-permute-start.14) | collective-permute-done | bytes 1048608 | tf_op jit(solution)/shard_map/ppermute | solution.py:50
  394.5 2.7 broadcast.22
  397.2 11.3 %constant_dynamic-update-slice_fusion.5 = (bf16[512,4096]{1,0:T(8,128)(2,1)}, bf16[512,1024]{1,0:T(8,128)(2,1)}, f32[512,1024]{1,0:T(8,128)}) fusion(bf16[512,4096]{1,0:T(8,128)(2,1)} %broadcast.22, s32[]{:T(128)S(6)} %select_n.14, s32[1024]{0:T(1024)S(1)} %iota_add_fusion, s32[512]{0:T(512)S(1)} %iota_add_fusion.1, ...), kind=kOutput, calls=%fused_computation.39 | convolution fusion | flops 4297588736 | bytes 16783364 | tf_op jit(solution)/shard_map/dot_general | solution.py:77
  409.5 1.4 collective-permute-start.16
  410.9 22.3 %collective-permute-done.15 = bf16[512,1024]{1,0:T(8,128)(2,1)} collective-permute-done((bf16[512,1024]{1,0:T(8,128)(2,1)}, bf16[512,1024]{1,0:T(8,128)(2,1)}, u32[]{:S(2)}, u32[]{:S(2)}) %collective-permute-start.15) | collective-permute-done | bytes 1048608 | tf_op jit(solution)/shard_map/ppermute | solution.py:50
  433.2 2.4 constant_dynamic-update-slice_fusion.4
  435.8 2.3 constant_dynamic-update-slice_fusion.3
  438.1 17.0 %collective-permute-done.17 = bf16[512,1024]{1,0:T(8,128)(2,1)S(1)} collective-permute-done((bf16[512,1024]{1,0:T(8,128)(2,1)}, bf16[512,1024]{1,0:T(8,128)(2,1)S(1)}, u32[]{:S(2)}, u32[]{:S(2)}) %collective-permute-start.17) | collective-permute-done | bytes 1048608 | tf_op jit(solution)/shard_map/ppermute | solution.py:50
  456.2 12.7 %all-gather.8.cloned.1.call-done = bf16[4096,1024]{1,0:T(8,128)(2,1)} async-done(((bf16[512,1024]{1,0:T(8,128)(2,1)}), bf16[4096,1024]{1,0:T(8,128)(2,1)}) %all-gather.8.cloned.1.call-update) | async-done | bytes 8388624 | tf_op jit(solution)/shard_map/all_gather | solution.py:88
  468.9 8.1 %fusion.23 = f32[512,1024]{1,0:T(8,128)S(1)} fusion(bf16[512,4096]{1,0:T(8,128)(2,1)} %constant_dynamic-update-slice_fusion.2, bf16[4096,1024]{1,0:T(8,128)(2,1)} %all-gather.8.cloned.1.call-done), kind=kOutput, calls=%fused_computation.64 | convolution fusion | flops 4294967296 | bytes 14680064 | tf_op jit(solution)/shard_map/dot_general | solution.py:81
  478.3 9.5 %collective-permute-start.18 = (f32[512,512]{1,0:T(8,128)}, f32[512,512]{1,0:T(8,128)}, u32[]{:S(2)}, u32[]{:S(2)}) collective-permute-start(f32[512,512]{1,0:T(8,128)} %get-tuple-element.15), channel_id=1, source_target_pairs={{0,0},{1,8},{2,16},{3,24},{4,4},{5,12},{6,20},{7,28},{8,1},{9,9},{... | collective-permute-start | bytes 3145736 | tf_op jit(solution)/shard_map/ppermute | solution.py:34
  488.3 5.3 fusion.16
  493.6 2.4 pad_maximum_fusion
  496.1 96.7 %psum.15 = f32[4]{0:T(128)S(1)} all-reduce(f32[4]{0:T(128)S(1)} %pad_maximum_fusion), channel_id=1, replica_groups=mesh['row'=8,'col'=4] {'row','col'}, use_global_device_ids=true, to_apply=%region_6.0 | all-reduce | flops 4 | bytes 32 | tf_op jit(solution)/shard_map/psum | solution.py:90
  593.2 1.6 copy.3
  594.8 1.6 copy.4
  596.9 1.3 copy-done.3
  (59 shorter events, 24.3 us)
Async XLA Ops:
  7.2 2.6 copy-start
  7.2 132.5 %all-gather.4.cloned.1.call-start = ((), (), s32[]{:S(2)}) async-start(), calls=%async_computation | async-start | bytes 9437184 | tf_op jit(solution)/shard_map/all_gather | solution.py:69
  11.5 321.5 %all-gather.6.cloned.1.call-start = ((), (), s32[]{:S(2)}) async-start(), calls=%async_computation.1 | async-start | bytes 9437184 | tf_op jit(solution)/shard_map/all_gather | solution.py:88
  11.5 89.3 %collective-permute-start = (bf16[512,1024]{1,0:T(8,128)(2,1)}, bf16[512,1024]{1,0:T(8,128)(2,1)}, u32[]{:S(2)}, u32[]{:S(2)}) collective-permute-start(bf16[512,1024]{1,0:T(8,128)(2,1)} %get-tuple-element.13), channel_id=1, source_target_pairs={{0,1},{1,2},{2,3},{3,0},{4,5},{5,6},{6,7},{7,4},{8,9},{9,10},{10,1... | collective-permute-start | bytes 3145736 | tf_op jit(solution)/shard_map/ppermute | solution.py:50
  12.0 91.3 %collective-permute-start.1 = (bf16[512,1024]{1,0:T(8,128)(2,1)}, bf16[512,1024]{1,0:T(8,128)(2,1)}, u32[]{:S(2)}, u32[]{:S(2)}) collective-permute-start(bf16[512,1024]{1,0:T(8,128)(2,1)} %get-tuple-element.13), channel_id=1, source_target_pairs={{0,2},{1,3},{2,0},{3,1},{4,6},{5,7},{6,4},{7,5},{8,10},{9,11},{10,... | collective-permute-start | bytes 3145736 | tf_op jit(solution)/shard_map/ppermute | solution.py:50
  14.6 91.0 %collective-permute-start.2 = (bf16[512,1024]{1,0:T(8,128)(2,1)}, bf16[512,1024]{1,0:T(8,128)(2,1)S(1)}, u32[]{:S(2)}, u32[]{:S(2)}) collective-permute-start(bf16[512,1024]{1,0:T(8,128)(2,1)} %get-tuple-element.13), channel_id=1, source_target_pairs={{0,3},{1,0},{2,1},{3,2},{4,7},{5,4},{6,5},{7,6},{8,11},{9,8},{10,9... | collective-permute-start | bytes 3145736 | tf_op jit(solution)/shard_map/ppermute | solution.py:50
  139.7 60.6 %slice-start = ((s8[8388608]{0:T(1024)(128)(4,1)}), s8[4194304]{0:T(1024)(128)(4,1)S(1)}, s32[]{:S(2)}) async-start(s8[8388608]{0:T(1024)(128)(4,1)} %bitcast.16), calls=%async_computation.3 | async-start | bytes 8388608
  140.2 60.1 %slice-start.1 = ((s8[8388608]{0:T(1024)(128)(4,1)}), s8[4194304]{0:T(1024)(128)(4,1)S(1)}, s32[]{:S(2)}) async-start(s8[8388608]{0:T(1024)(128)(4,1)} %bitcast.16), calls=%async_computation.4 | async-start | bytes 8388608
  152.8 24.9 %collective-permute-start.3 = (bf16[512,1024]{1,0:T(8,128)(2,1)S(1)}, bf16[512,1024]{1,0:T(8,128)(2,1)S(1)}, u32[]{:S(2)}, u32[]{:S(2)}) collective-permute-start(bf16[512,1024]{1,0:T(8,128)(2,1)S(1)} %get-tuple-element.11), channel_id=1, source_target_pairs={{0,1},{1,2},{2,3},{3,0},{4,5},{5,6},{6,7},{7,4},{8,9},{9,10},{10,1... | collective-permute-start | bytes 3145736 | tf_op jit(solution)/shard_map/ppermute | solution.py:50
  152.8 26.0 %collective-permute-start.4 = (bf16[512,1024]{1,0:T(8,128)(2,1)S(1)}, bf16[512,1024]{1,0:T(8,128)(2,1)S(1)}, u32[]{:S(2)}, u32[]{:S(2)}) collective-permute-start(bf16[512,1024]{1,0:T(8,128)(2,1)S(1)} %get-tuple-element.11), channel_id=1, source_target_pairs={{0,2},{1,3},{2,0},{3,1},{4,6},{5,7},{6,4},{7,5},{8,10},{9,11},{10,... | collective-permute-start | bytes 3145736 | tf_op jit(solution)/shard_map/ppermute | solution.py:50
  154.2 45.4 %collective-permute-start.5 = (bf16[512,1024]{1,0:T(8,128)(2,1)S(1)}, bf16[512,1024]{1,0:T(8,128)(2,1)S(1)}, u32[]{:S(2)}, u32[]{:S(2)}) collective-permute-start(bf16[512,1024]{1,0:T(8,128)(2,1)S(1)} %get-tuple-element.11), channel_id=1, source_target_pairs={{0,3},{1,0},{2,1},{3,2},{4,7},{5,4},{6,5},{7,6},{8,11},{9,8},{10,9... | collective-permute-start | bytes 3145736 | tf_op jit(solution)/shard_map/ppermute | solution.py:50
  207.6 2.0 copy-start.1
  209.6 259.3 %all-gather.8.cloned.1.call-start = ((), (), s32[]{:S(2)}) async-start(), calls=%async_computation.2 | async-start | bytes 9437184 | tf_op jit(solution)/shard_map/all_gather | solution.py:88
  209.6 24.5 %collective-permute-start.6 = (bf16[512,1024]{1,0:T(8,128)(2,1)}, bf16[512,1024]{1,0:T(8,128)(2,1)S(1)}, u32[]{:S(2)}, u32[]{:S(2)}) collective-permute-start(bf16[512,1024]{1,0:T(8,128)(2,1)} %get-tuple-element.18), channel_id=1, source_target_pairs={{0,1},{1,2},{2,3},{3,0},{4,5},{5,6},{6,7},{7,4},{8,9},{9,10},{10,1... | collective-permute-start | bytes 3145736 | tf_op jit(solution)/shard_map/ppermute | solution.py:50
  210.6 26.2 %collective-permute-start.7 = (bf16[512,1024]{1,0:T(8,128)(2,1)}, bf16[512,1024]{1,0:T(8,128)(2,1)S(1)}, u32[]{:S(2)}, u32[]{:S(2)}) collective-permute-start(bf16[512,1024]{1,0:T(8,128)(2,1)} %get-tuple-element.18), channel_id=1, source_target_pairs={{0,2},{1,3},{2,0},{3,1},{4,6},{5,7},{6,4},{7,5},{8,10},{9,11},{10,... | collective-permute-start | bytes 3145736 | tf_op jit(solution)/shard_map/ppermute | solution.py:50
  212.0 44.3 %collective-permute-start.8 = (bf16[512,1024]{1,0:T(8,128)(2,1)}, bf16[512,1024]{1,0:T(8,128)(2,1)S(1)}, u32[]{:S(2)}, u32[]{:S(2)}) collective-permute-start(bf16[512,1024]{1,0:T(8,128)(2,1)} %get-tuple-element.18), channel_id=1, source_target_pairs={{0,3},{1,0},{2,1},{3,2},{4,7},{5,4},{6,5},{7,6},{8,11},{9,8},{10,9... | collective-permute-start | bytes 3145736 | tf_op jit(solution)/shard_map/ppermute | solution.py:50
  257.4 3.8 copy-start.2
  271.1 23.3 %collective-permute-start.9 = (bf16[512,1024]{1,0:T(8,128)(2,1)S(1)}, bf16[512,1024]{1,0:T(8,128)(2,1)S(1)}, u32[]{:S(2)}, u32[]{:S(2)}) collective-permute-start(bf16[512,1024]{1,0:T(8,128)(2,1)S(1)} %get-tuple-element.9), channel_id=1, source_target_pairs={{0,1},{1,2},{2,3},{3,0},{4,5},{5,6},{6,7},{7,4},{8,9},{9,10},{10,1... | collective-permute-start | bytes 3145736 | tf_op jit(solution)/shard_map/ppermute | solution.py:50
  272.7 26.0 %collective-permute-start.10 = (bf16[512,1024]{1,0:T(8,128)(2,1)S(1)}, bf16[512,1024]{1,0:T(8,128)(2,1)S(1)}, u32[]{:S(2)}, u32[]{:S(2)}) collective-permute-start(bf16[512,1024]{1,0:T(8,128)(2,1)S(1)} %get-tuple-element.9), channel_id=1, source_target_pairs={{0,2},{1,3},{2,0},{3,1},{4,6},{5,7},{6,4},{7,5},{8,10},{9,11},{10,... | collective-permute-start | bytes 3145736 | tf_op jit(solution)/shard_map/ppermute | solution.py:50
  273.2 44.9 %collective-permute-start.11 = (bf16[512,1024]{1,0:T(8,128)(2,1)S(1)}, bf16[512,1024]{1,0:T(8,128)(2,1)S(1)}, u32[]{:S(2)}, u32[]{:S(2)}) collective-permute-start(bf16[512,1024]{1,0:T(8,128)(2,1)S(1)} %get-tuple-element.9), channel_id=1, source_target_pairs={{0,3},{1,0},{2,1},{3,2},{4,7},{5,4},{6,5},{7,6},{8,11},{9,8},{10,9... | collective-permute-start | bytes 3145736 | tf_op jit(solution)/shard_map/ppermute | solution.py:50
  346.1 25.1 %collective-permute-start.12 = (bf16[512,1024]{1,0:T(8,128)(2,1)}, bf16[512,1024]{1,0:T(8,128)(2,1)S(1)}, u32[]{:S(2)}, u32[]{:S(2)}) collective-permute-start(bf16[512,1024]{1,0:T(8,128)(2,1)} %get-tuple-element.21), channel_id=1, source_target_pairs={{0,1},{1,2},{2,3},{3,0},{4,5},{5,6},{6,7},{7,4},{8,9},{9,10},{10,1... | collective-permute-start | bytes 3145736 | tf_op jit(solution)/shard_map/ppermute | solution.py:50
  346.1 26.3 %collective-permute-start.13 = (bf16[512,1024]{1,0:T(8,128)(2,1)}, bf16[512,1024]{1,0:T(8,128)(2,1)S(1)}, u32[]{:S(2)}, u32[]{:S(2)}) collective-permute-start(bf16[512,1024]{1,0:T(8,128)(2,1)} %get-tuple-element.21), channel_id=1, source_target_pairs={{0,2},{1,3},{2,0},{3,1},{4,6},{5,7},{6,4},{7,5},{8,10},{9,11},{10,... | collective-permute-start | bytes 3145736 | tf_op jit(solution)/shard_map/ppermute | solution.py:50
  347.7 45.7 %collective-permute-start.14 = (bf16[512,1024]{1,0:T(8,128)(2,1)}, bf16[512,1024]{1,0:T(8,128)(2,1)S(1)}, u32[]{:S(2)}, u32[]{:S(2)}) collective-permute-start(bf16[512,1024]{1,0:T(8,128)(2,1)} %get-tuple-element.21), channel_id=1, source_target_pairs={{0,3},{1,0},{2,1},{3,2},{4,7},{5,4},{6,5},{7,6},{8,11},{9,8},{10,9... | collective-permute-start | bytes 3145736 | tf_op jit(solution)/shard_map/ppermute | solution.py:50
  408.5 24.6 %collective-permute-start.15 = (bf16[512,1024]{1,0:T(8,128)(2,1)}, bf16[512,1024]{1,0:T(8,128)(2,1)}, u32[]{:S(2)}, u32[]{:S(2)}) collective-permute-start(bf16[512,1024]{1,0:T(8,128)(2,1)} %get-tuple-element.7), channel_id=1, source_target_pairs={{0,1},{1,2},{2,3},{3,0},{4,5},{5,6},{6,7},{7,4},{8,9},{9,10},{10,1... | collective-permute-start | bytes 3145736 | tf_op jit(solution)/shard_map/ppermute | solution.py:50
  409.5 26.3 %collective-permute-start.16 = (bf16[512,1024]{1,0:T(8,128)(2,1)}, bf16[512,1024]{1,0:T(8,128)(2,1)}, u32[]{:S(2)}, u32[]{:S(2)}) collective-permute-start(bf16[512,1024]{1,0:T(8,128)(2,1)} %get-tuple-element.7), channel_id=1, source_target_pairs={{0,2},{1,3},{2,0},{3,1},{4,6},{5,7},{6,4},{7,5},{8,10},{9,11},{10,... | collective-permute-start | bytes 3145736 | tf_op jit(solution)/shard_map/ppermute | solution.py:50
  410.9 44.3 %collective-permute-start.17 = (bf16[512,1024]{1,0:T(8,128)(2,1)}, bf16[512,1024]{1,0:T(8,128)(2,1)S(1)}, u32[]{:S(2)}, u32[]{:S(2)}) collective-permute-start(bf16[512,1024]{1,0:T(8,128)(2,1)} %get-tuple-element.7), channel_id=1, source_target_pairs={{0,3},{1,0},{2,1},{3,2},{4,7},{5,4},{6,5},{7,6},{8,11},{9,8},{10,9... | collective-permute-start | bytes 3145736 | tf_op jit(solution)/shard_map/ppermute | solution.py:50
  478.3 115.0 %collective-permute-start.18 = (f32[512,512]{1,0:T(8,128)}, f32[512,512]{1,0:T(8,128)}, u32[]{:S(2)}, u32[]{:S(2)}) collective-permute-start(f32[512,512]{1,0:T(8,128)} %get-tuple-element.15), channel_id=1, source_target_pairs={{0,0},{1,8},{2,16},{3,24},{4,4},{5,12},{6,20},{7,28},{8,1},{9,9},{... | collective-permute-start | bytes 3145736 | tf_op jit(solution)/shard_map/ppermute | solution.py:34
  487.7 107.1 %collective-permute-start.19 = (f32[512,512]{1,0:T(8,128)S(1)}, f32[512,512]{1,0:T(8,128)}, u32[]{:S(2)}, u32[]{:S(2)}) collective-permute-start(f32[512,512]{1,0:T(8,128)S(1)} %get-tuple-element.14), channel_id=1, source_target_pairs={{0,4},{1,12},{2,20},{3,28},{4,0},{5,8},{6,16},{7,24},{8,5},{9,13},... | collective-permute-start | bytes 3145736 | tf_op jit(solution)/shard_map/ppermute | solution.py:34
  596.9 1.3 copy-start.3
Sparse Core Ops, SparseCore 0:
  11.6 128.0 all-gather.3
  209.7 123.2 all-gather.5
  346.2 122.6 all-gather.7
